TPU v7x, 32 devices: a whole 2x2x4 slice. The times are simulated.
32 devices in a mesh: row: 4 (over y, x), col: 4 (over z), crop: 2 (over core).
Axes of the slice: x: 2, y: 2, z: 4, core: 2. Of those that a mesh axis runs over, the one named last changes fastest.
Arguments:
- pair_repr: bfloat16 [256, 128, 128], P(('crop', 'row'), 'col'), parts along dimension 0, may hold values from -6 to 6
- pair_mask: int32 [256, 128], P(('crop', 'row'), 'col'), parts along dimension 0, may hold values 0 or 1
- out_left_w: bfloat16 [128, 256], replicated, may hold values from -0.5 to 0.5
- out_right_w: bfloat16 [128, 256], replicated, may hold values from -0.5 to 0.5
- out_gate_w: bfloat16 [128, 128], replicated, may hold values from -0.5 to 0.5
- out_final_w: bfloat16 [128, 128], replicated, may hold values from -0.5 to 0.5
- in_left_w: bfloat16 [128, 256], replicated, may hold values from -0.5 to 0.5
- in_right_w: bfloat16 [128, 256], replicated, may hold values from -0.5 to 0.5
- in_gate_w: bfloat16 [128, 128], replicated, may hold values from -0.5 to 0.5
- in_final_w: bfloat16 [128, 128], replicated, may hold values from -0.5 to 0.5
- trans_in_w: bfloat16 [128, 1024], replicated, may hold values from -0.5 to 0.5
- trans_out_w: bfloat16 [512, 128], replicated, may hold values from -0.25 to 0.25
Outputs:
- pair_out: bfloat16 [256, 128, 128], P(('crop', 'row'), 'col'), parts along dimension 0
There are 2 independent parts, one for each index of `crop`. A program takes and returns all parts, laid end to end along the dimension named above; an argument that names none is the same for every part. Nothing has to cross between parts.
All inputs are finite; a program needn't handle non-finite values. No bound on the sum of `pair_mask` on one device may be relied on, other than what follows from the above.
Results may differ from a plain program's by a relative error of at most 0.015.
Values may be sent and summed in bfloat16 or wider, within the bound.
No kernel may reach another device: no remote copies, remote signals or barrier semaphores. Data moves between devices by JAX's collectives and lax.ppermute only.
A program may use at most 128 MiB of HBM per device.

v0:
```python
import jax
import jax.numpy as jnp
from jax import lax
from jax.sharding import PartitionSpec as P

epsilon = 1e-05


def layer_norm(values):
    average = jnp.mean(values, axis=-1, keepdims=True)
    centered = values - average
    spread = jnp.mean(centered * centered, axis=-1, keepdims=True)
    return centered * lax.rsqrt(spread + epsilon)


def gated(normed, weight, mask_vals):
    projected = jnp.dot(normed, weight, preferred_element_type=jnp.float32)
    half_width = weight.shape[1] // 2
    result = jax.nn.sigmoid(projected[..., :half_width]) * projected[..., half_width:]
    result = result * mask_vals[..., None]
    return result.astype(jnp.bfloat16)


def finish(pair_repr, normed, triangle, gate_w, final_w):
    gate_vals = jax.nn.sigmoid(jnp.dot(normed, gate_w, preferred_element_type=jnp.float32))
    tri_norm = layer_norm(triangle).astype(jnp.bfloat16)
    update = jnp.dot(tri_norm, final_w, preferred_element_type=jnp.float32)
    return (pair_repr.astype(jnp.float32) + gate_vals * update).astype(jnp.bfloat16)


def shards(
    pair_repr,
    pair_mask,
    out_left_w,
    out_right_w,
    out_gate_w,
    out_final_w,
    in_left_w,
    in_right_w,
    in_gate_w,
    in_final_w,
    trans_in_w,
    trans_out_w,
):
    mask_vals = pair_mask.astype(jnp.float32)
    normed_out = layer_norm(pair_repr.astype(jnp.float32)).astype(jnp.bfloat16)
    outbound = gated(normed_out, out_right_w, mask_vals)
    turned_right = lax.all_to_all(
        lax.all_to_all(outbound, "row", split_axis=0, concat_axis=0, tiled=True),
        "col",
        split_axis=0,
        concat_axis=1,
        tiled=True,
    )
    left_tile = gated(normed_out, out_left_w, mask_vals)
    gathered = lax.all_gather(left_tile, "col", axis=1, tiled=True)
    triangle = jnp.einsum(
        "ikh,jkh->ijh",
        gathered,
        lax.all_gather(turned_right, "row", axis=0, tiled=True),
        preferred_element_type=jnp.float32,
    )
    middle = finish(pair_repr, normed_out, triangle, out_gate_w, out_final_w)
    normed_in = layer_norm(middle.astype(jnp.float32)).astype(jnp.bfloat16)
    outbound_left = gated(normed_in, in_left_w, mask_vals)
    turned_left = lax.all_to_all(
        lax.all_to_all(outbound_left, "col", split_axis=1, concat_axis=1, tiled=True),
        "row",
        split_axis=1,
        concat_axis=0,
        tiled=True,
    )
    right_tile = gated(normed_in, in_right_w, mask_vals)
    column_panel = lax.all_gather(right_tile, "row", axis=0, tiled=True)
    triangle_in = jnp.einsum(
        "kih,kjh->ijh",
        lax.all_gather(turned_left, "col", axis=1, tiled=True),
        column_panel,
        preferred_element_type=jnp.float32,
    )
    after_in = finish(middle, normed_in, triangle_in, in_gate_w, in_final_w)
    normed_mix = layer_norm(after_in.astype(jnp.float32)).astype(jnp.bfloat16)
    projected = jnp.dot(normed_mix, trans_in_w, preferred_element_type=jnp.float32)
    half_width = trans_in_w.shape[1] // 2
    hidden = (jax.nn.silu(projected[..., :half_width]) * projected[..., half_width:]).astype(
        jnp.bfloat16
    )
    result = after_in.astype(jnp.float32) + jnp.dot(
        hidden, trans_out_w, preferred_element_type=jnp.float32
    )
    return result.astype(jnp.bfloat16)


def solution(mesh):
    in_specs = (
        P(("crop", "row"), "col", None),
        P(("crop", "row"), "col"),
        P(),
        P(),
        P(),
        P(),
        P(),
        P(),
        P(),
        P(),
        P(),
        P(),
    )
    out_specs = P(("crop", "row"), "col", None)
    return jax.shard_map(shards, mesh=mesh, in_specs=in_specs, out_specs=out_specs, check_vma=False)
```

profile of v0, /device:TPU:0, one launch (start us, length us, event | category | flops | bytes accessed | tf_op | source)
XLA Modules:
  0.0 162.0 jit_solution(13725264176336256992)
XLA Ops:
  6.5 0.0 copy-start
  6.5 1.2 convert_reduce_fusion
  7.8 1.3 fusion.17
  9.1 1.4 fusion.44
  10.6 1.3 fusion.46
  11.9 0.0 copy-done.6
  11.9 0.0 copy-start.8
  11.9 1.0 fusion.30
  12.9 0.0 all-gather.7.cloned.1.call-update
  12.9 0.0 all-gather.5.cloned.1.call-start
  13.0 10.7 %all_to_all.46 = bf16[32,32,128]{2,1,0:T(8,128)(2,1)S(1)} all-to-all(bf16[32,32,128]{2,1,0:T(8,128)(2,1)S(1)} %get-tuple-element.8), channel_id=1, replica_groups=mesh['row'=4,'col'=4,'crop'=2] {'row'}, dimensions={0} | all-to-all | bytes 524288 | tf_op jit(solution)/shard_map/all_to_all | solution.py:49
  23.7 21.0 %all_to_all.47 = bf16[32,32,128]{2,1,0:T(8,128)(2,1)S(1)} all-to-all(bf16[32,32,128]{2,1,0:T(8,128)(2,1)S(1)} %all_to_all.46), channel_id=1, replica_groups=mesh['row'=4,'col'=4,'crop'=2] {'col'}, dimensions={0} | all-to-all | bytes 524288 | tf_op jit(solution)/shard_map/all_to_all | solution.py:48
  44.7 0.9 copy.66
  45.6 0.0 all-gather.5.cloned.1.call-update
  45.7 0.0 all-gather.9.cloned.1.call-start
  45.7 0.0 copy-done.8
  45.7 0.7 fusion.6
  46.5 3.4 %all-gather.7.cloned.1.call-done = bf16[32,128,128]{2,1,0:T(8,128)(2,1)} async-done(((bf16[32,32,128]{2,1,0:T(8,128)(2,1)}), bf16[32,128,128]{2,1,0:T(8,128)(2,1)}) %all-gather.7.cloned.1.call-update) | async-done | bytes 1048592 | tf_op jit(solution)/shard_map/all_gather | solution.py:56
  49.9 2.7 %copy.67 = bf16[32,128,128]{1,0,2:T(8,128)(2,1)} copy(bf16[32,128,128]{2,1,0:T(8,128)(2,1)} %all-gather.7.cloned.1.call-done) | data formatting | bytes 2097152 | tf_op jit(solution)/shard_map/all_gather | solution.py:56
  52.5 24.4 %all-gather.5.cloned.1.call-done = bf16[32,128,128]{1,0,2:T(8,128)(2,1)} async-done(((bf16[8,128,128]{1,0,2:T(8,128)(2,1)}), bf16[32,128,128]{1,0,2:T(8,128)(2,1)}) %all-gather.5.cloned.1.call-update) | async-done | bytes 1048592 | tf_op jit(solution)/shard_map/all_gather | solution.py:60
  76.9 2.2 %bitcast_reduce_fusion.1 = (f32[32,32]{0,1:T(8,128)S(1)}, f32[128,32,32]{2,1,0:T(8,128)S(1)}) fusion(bf16[32,128,128]{1,0,2:T(8,128)(2,1)} %all-gather.5.cloned.1.call-done, bf16[32,128,128]{1,0,2:T(8,128)(2,1)} %copy.67), kind=kOutput, calls=%fused_computation.5 | convolution fusion | flops 33684480 | bytes 2625536 | tf_op jit(solution)/shard_map/ikh,jkh->ijh/dot_general | solution.py:57
  79.2 0.1 copy.68
  79.2 0.1 copy.69
  79.3 0.3 multiply_reduce_fusion.1
  79.6 0.1 copy.70
  79.7 0.1 copy.71
  79.8 1.3 multiply_convert_fusion.1
  81.1 2.7 %copy.72 = bf16[32,32,128]{2,1,0:T(8,128)(2,1)S(1)} copy(bf16[32,32,128]{0,1,2:T(8,128)(2,1)} %multiply_convert_fusion.1) | data formatting | bytes 524288 | tf_op jit(solution)/shard_map/convert_element_type | solution.py:26
  83.7 0.0 copy-start.3
  83.8 0.4 fusion.60
  84.1 0.4 multiply_reduce_fusion.3
  84.5 0.3 multiply_convert_fusion.3
  84.9 0.3 fusion.49
  85.2 0.0 copy-done.3
  85.2 0.3 fusion.51
  85.5 1.0 fusion.20
  86.5 0.0 all-gather.9.cloned.1.call-update
  86.5 0.0 all-gather.11.cloned.1.call-start
  86.5 0.1 copy.73
  86.7 13.1 %all_to_all.48 = bf16[32,32,128]{2,0,1:T(8,128)(2,1)S(1)} all-to-all(bf16[32,32,128]{2,0,1:T(8,128)(2,1)S(1)} %copy.73), channel_id=1, replica_groups=mesh['row'=4,'col'=4,'crop'=2] {'col'}, dimensions={1} | all-to-all | bytes 524288 | tf_op jit(solution)/shard_map/all_to_all | solution.py:67
  99.8 8.2 %all_to_all.49 = bf16[32,32,128]{2,0,1:T(8,128)(2,1)S(1)} all-to-all(bf16[32,32,128]{2,0,1:T(8,128)(2,1)S(1)} %all_to_all.48), channel_id=1, replica_groups=mesh['row'=4,'col'=4,'crop'=2] {'row'}, dimensions={1} | all-to-all | bytes 524288 | tf_op jit(solution)/shard_map/all_to_all | solution.py:66
  108.0 0.1 copy.75
  108.1 0.9 copy.76
  109.0 0.0 all-gather.11.cloned.1.call-update
  109.1 1.1 fusion.3
  110.2 3.4 %all-gather.9.cloned.1.call-done = bf16[128,32,128]{2,1,0:T(8,128)(2,1)} async-done(((bf16[32,32,128]{2,1,0:T(8,128)(2,1)}), bf16[128,32,128]{2,1,0:T(8,128)(2,1)}) %all-gather.9.cloned.1.call-update) | async-done | bytes 1048592 | tf_op jit(solution)/shard_map/all_gather | solution.py:74
  113.6 3.2 %copy.77 = bf16[128,32,128]{0,1,2:T(8,128)(2,1)} copy(bf16[128,32,128]{2,1,0:T(8,128)(2,1)} %all-gather.9.cloned.1.call-done) | data formatting | bytes 2097152 | tf_op jit(solution)/shard_map/all_gather | solution.py:74
  116.8 27.7 %all-gather.11.cloned.1.call-done = bf16[128,32,128]{0,1,2:T(8,128)(2,1)} async-done(((bf16[128,8,128]{0,1,2:T(8,128)(2,1)}), bf16[128,32,128]{0,1,2:T(8,128)(2,1)}) %all-gather.11.cloned.1.call-update) | async-done | bytes 1048592 | tf_op jit(solution)/shard_map/all_gather | solution.py:77
  144.5 2.2 %bitcast_reduce_fusion = (f32[32,32]{0,1:T(8,128)S(1)}, f32[128,32,32]{2,1,0:T(8,128)S(1)}) fusion(bf16[128,32,128]{0,1,2:T(8,128)(2,1)} %copy.77, bf16[128,32,128]{0,1,2:T(8,128)(2,1)} %all-gather.11.cloned.1.call-done), kind=kOutput, calls=%fused_computation.3 | convolution fusion | flops 33684480 | bytes 2625536 | tf_op jit(solution)/shard_map/kih,kjh->ijh/dot_general | solution.py:75
  146.7 0.1 copy.78
  146.8 0.1 copy.79
  146.9 0.3 multiply_reduce_fusion
  147.2 0.1 copy.80
  147.3 0.1 copy.81
  147.4 1.3 multiply_convert_fusion
  148.6 2.6 %copy.82 = bf16[32,32,128]{2,1,0:T(8,128)(2,1)S(1)} copy(bf16[32,32,128]{0,1,2:T(8,128)(2,1)} %multiply_convert_fusion) | data formatting | bytes 524288 | tf_op jit(solution)/shard_map/convert_element_type | solution.py:26
  151.3 0.0 copy-done.4
  151.3 1.4 fusion.61
  152.7 0.4 multiply_reduce_fusion.2
  153.1 0.0 copy-done
  153.1 0.0 copy-start.7
  153.1 0.8 fusion.39
  153.9 0.1 copy-done.7
  154.0 1.4 fusion.13
  (23 shorter events, 0.1 us)
Async XLA Ops:
  6.5 146.6 %copy-start = (bf16[128,1024]{1,0:T(8,128)(2,1)S(1)}, bf16[128,1024]{1,0:T(8,128)(2,1)}, u32[]{:S(2)}) copy-start(bf16[128,1024]{1,0:T(8,128)(2,1)} %param.22) | copy-start | bytes 786436
  6.5 4.0 %copy-start.1 = (bf16[32,32,128]{2,1,0:T(8,128)(2,1)S(1)}, bf16[32,32,128]{2,1,0:T(8,128)(2,1)}, u32[]{:S(2)}) copy-start(bf16[32,32,128]{2,1,0:T(8,128)(2,1)} %param.12) | copy-start | bytes 786436
  6.5 5.3 %copy-start.6 = (s32[32,32]{1,0:T(8,128)S(1)}, s32[32,32]{1,0:T(8,128)}, u32[]{:S(2)}) copy-start(s32[32,32]{1,0:T(8,128)} %param.13) | copy-start | bytes 12292
  6.5 43.3 %all-gather.7.cloned.1.call-start = ((), (), s32[]{:S(2)}) async-start(), calls=%async_computation.5 | async-start | bytes 1310720 | tf_op jit(solution)/shard_map/all_gather | solution.py:56
  11.9 33.8 %copy-start.8 = (bf16[128,128]{1,0:T(8,128)(2,1)S(1)}, bf16[128,128]{1,0:T(8,128)(2,1)}, u32[]{:S(2)}) copy-start(bf16[128,128]{1,0:T(8,128)(2,1)} %param.16) | copy-start | bytes 98308
  12.9 64.0 %all-gather.5.cloned.1.call-start = ((), (), s32[]{:S(2)}) async-start(), calls=%async_computation.4 | async-start | bytes 1310720 | tf_op jit(solution)/shard_map/all_gather | solution.py:60
  45.7 67.9 %all-gather.9.cloned.1.call-start = ((), (), s32[]{:S(2)}) async-start(), calls=%async_computation.6 | async-start | bytes 1310720 | tf_op jit(solution)/shard_map/all_gather | solution.py:74
  79.8 3.9 %copy-start.5 = (bf16[128,128]{1,0:T(8,128)(2,1)S(1)}, bf16[128,128]{1,0:T(8,128)(2,1)}, u32[]{:S(2)}) copy-start(bf16[128,128]{1,0:T(8,128)(2,1)} %param.17) | copy-start | bytes 98308
  81.1 3.8 %copy-start.2 = (bf16[128,256]{1,0:T(8,128)(2,1)S(1)}, bf16[128,256]{1,0:T(8,128)(2,1)}, u32[]{:S(2)}) copy-start(bf16[128,256]{1,0:T(8,128)(2,1)} %param.18) | copy-start | bytes 196612
  83.7 1.4 copy-start.3
  86.5 22.6 %copy-start.9 = (bf16[128,128]{1,0:T(8,128)(2,1)S(1)}, bf16[128,128]{1,0:T(8,128)(2,1)}, u32[]{:S(2)}) copy-start(bf16[128,128]{1,0:T(8,128)(2,1)} %param.20) | copy-start | bytes 98308
  86.5 58.0 %all-gather.11.cloned.1.call-start = ((), (), s32[]{:S(2)}) async-start(), calls=%async_computation.7 | async-start | bytes 1310720 | tf_op jit(solution)/shard_map/all_gather | solution.py:77
  147.4 3.9 %copy-start.4 = (bf16[128,128]{1,0:T(8,128)(2,1)S(1)}, bf16[128,128]{1,0:T(8,128)(2,1)}, u32[]{:S(2)}) copy-start(bf16[128,128]{1,0:T(8,128)(2,1)} %param.21) | copy-start | bytes 98308
  153.1 0.9 copy-start.7
Sparse Core Ops, SparseCore 0:
  13.1 36.7 all-gather.6
  51.7 25.2 all-gather.4
  86.6 26.9 all-gather.8
  115.0 29.4 all-gather.10
where the time goes:
time: 163 us; the launch traced here: 162 us
  waiting for transfers between devices  59 us (36%)
  blocking collectives  53.1 us (33%)
  local copies, waits for them, and re-layouts  14 us (9%)
  matrix products  13.4 us (8%)
  between operations  13.4 us (8%)
  other arithmetic  8.94 us (5%)
    all_gather x1, waiting for transfers between devices, shards(): lax.all_gather(turned_left, 'col', axis=1, tiled=True)  27.7 us
    all_gather x1, waiting for transfers between devices, shards(): lax.all_gather(turned_right, 'row', axis=0, tiled=True)  24.4 us
    all_to_all x1, blocking collectives, shards(): lax.all_to_all(lax.all_to_all(outbound, 'row', split_axis=0, concat_axis=...  21 us
    all_to_all x1, blocking collectives, shards(): lax.all_to_all(outbound_left, 'col', split_axis=1, concat_axis=1, tiled=T...  13.1 us
    all_to_all x1, blocking collectives, shards(): lax.all_to_all(outbound, 'row', split_axis=0, concat_axis=0, tiled=True)  10.7 us
    all_to_all x1, blocking collectives, shards(): lax.all_to_all(lax.all_to_all(outbound_left, 'col', split_axis=1, concat_...  8.25 us
    convert_element_type x2, local copies, waits for them, and re-layouts, finish(): tri_norm = layer_norm(triangle).astype(jnp.bfloat16)  5.27 us
    all_gather x1, waiting for transfers between devices, shards(): column_panel = lax.all_gather(right_tile, 'row', axis=0, tiled=True)  3.41 us
  transfers between devices with their start and end apart: 4, of which 4 were waited for; matrix products, arithmetic and copies ran while one was open for 6% of the time, Pallas kernels for 0%

commit v1 on v0

--- a/solution.py
+++ b/solution.py
@@ -72,11 +72,31 @@
     )
     right_tile = gated(normed_in, in_right_w, mask_vals)
     column_panel = lax.all_gather(right_tile, "row", axis=0, tiled=True)
-    triangle_in = jnp.einsum(
-        "kih,kjh->ijh",
-        lax.all_gather(turned_left, "col", axis=1, tiled=True),
-        column_panel,
-        preferred_element_type=jnp.float32,
+
+    def _wrap_words(here_x, panel):
+        outer = lax.axis_index("col")
+        val = lax.axis_size("col")
+        low, then, ready = (val, outer, here_x.shape[1])
+        latest, local_part = ([], [])
+        frame_out = d_next = here_x
+        for s in [*range(low // 2 + 1)]:
+            z2 = panel(frame_out, (then - s) % low * ready)
+            latest.append(z2)
+            if 0 < s < low - low // 2:
+                local_part.append(panel(d_next, (then + s) % low * ready))
+            frame_out = lax.ppermute(frame_out, "col", [(rr, (rr + 1) % low) for rr in range(low)])
+            d_next = lax.ppermute(d_next, "col", [(rr, (rr - 1) % low) for rr in range(low)])
+        return jnp.roll(
+            jnp.concatenate([*latest[::-1], *local_part], axis=0),
+            (then - low // 2) * latest[0].shape[0],
+            axis=0,
+        )
+
+    triangle_in = _wrap_words(
+        turned_left,
+        panel=lambda shard, start: jnp.einsum(
+            "kih,kjh->ijh", shard, column_panel, preferred_element_type=jnp.float32
+        ),
     )
     after_in = finish(middle, normed_in, triangle_in, in_gate_w, in_final_w)
     normed_mix = layer_norm(after_in.astype(jnp.float32)).astype(jnp.bfloat16)

time: 163 us -> 150 us (0.920)
  waiting for transfers between devices: 59 us -> 32.2 us
  matrix products: 13.4 us -> 23 us
  starting transfers between devices: 0.13 us -> 4.34 us
    all_gather x1 -> x0, waiting for transfers between devices: 27.7 us -> none  [shards(): lax.all_gather(turned_left, 'col', axis=1, tiled=True)]
    dot_general x1 -> x4, matrix products: 2.2 us -> 11.5 us  [shards(): jnp.einsum('kih,kjh->ijh', shard, column_panel, preferred_element_type=jn...]
    ppermute x0 -> x3, waiting for transfers between devices: none -> 4.8 us  [the longest x2 4.8 us: _wrap_words(): lax.ppermute(frame_out, 'col', [(rr, (rr + 1) % low) for rr in range(low)])]
    ppermute x0 -> x3, starting transfers between devices: none -> 4.25 us  [the longest x1 3.76 us: _wrap_words(): lax.ppermute(d_next, 'col', [(rr, (rr - 1) % low) for rr in range(low)])]
    all_gather x1, local copies, waits for them, and re-layouts: 3.2 us -> 7.25 us  [shards(): column_panel = lax.all_gather(right_tile, 'row', axis=0, tiled=True)]
    all_gather x1, waiting for transfers between devices: 3.41 us -> 0.01 us  [shards(): column_panel = lax.all_gather(right_tile, 'row', axis=0, tiled=True)]
    convert_element_type x2 -> x1, local copies, waits for them, and re-layouts: 5.27 us -> 2.65 us  [finish(): tri_norm = layer_norm(triangle).astype(jnp.bfloat16)]
  transfers between devices with their start and end apart: 4 -> 6, of which waited for: 4 -> 3; matrix products, arithmetic and copies ran while one was open for 6% -> 14% of each run, Pallas kernels for 0% -> 0%
where the time goes in v1:
time: 150 us; the launch traced here: 149 us
  blocking collectives  53.2 us (35%)
  waiting for transfers between devices  32.2 us (21%)
  matrix products  23 us (15%)
  local copies, waits for them, and re-layouts  15.3 us (10%)
  between operations  13.5 us (9%)
  other arithmetic  7.92 us (5%)
  starting transfers between devices  4.34 us (3%)
    all_gather x1, waiting for transfers between devices, shards(): lax.all_gather(turned_right, 'row', axis=0, tiled=True)  24.4 us
    all_to_all x1, blocking collectives, shards(): lax.all_to_all(lax.all_to_all(outbound, 'row', split_axis=0, concat_axis=...  21 us
    all_to_all x1, blocking collectives, shards(): lax.all_to_all(outbound_left, 'col', split_axis=1, concat_axis=1, tiled=T...  13.1 us
    dot_general x4, matrix products, shards(): jnp.einsum('kih,kjh->ijh', shard, column_panel, preferred_element_type=jn...  11.5 us
    all_to_all x1, blocking collectives, shards(): lax.all_to_all(outbound, 'row', split_axis=0, concat_axis=0, tiled=True)  10.7 us
    all_to_all x1, blocking collectives, shards(): lax.all_to_all(lax.all_to_all(outbound_left, 'col', split_axis=1, concat_...  8.36 us
    all_gather x1, local copies, waits for them, and re-layouts, shards(): column_panel = lax.all_gather(right_tile, 'row', axis=0, tiled=True)  7.25 us
    ppermute x2, waiting for transfers between devices, _wrap_words(): lax.ppermute(frame_out, 'col', [(rr, (rr + 1) % low) for rr in range(low)])  4.8 us
  transfers between devices with their start and end apart: 6, of which 3 were waited for; matrix products, arithmetic and copies ran while one was open for 14% of the time, Pallas kernels for 0%

profile of v1, /device:TPU:0, one launch (start us, length us, event | category | flops | bytes accessed | tf_op | source)
XLA Modules:
  0.0 149.4 jit_solution(8989359740015627291)
XLA Ops:
  6.5 1.2 convert_reduce_fusion
  7.8 1.3 fusion.17
  9.1 1.4 fusion.46
  10.6 1.3 fusion.48
  11.9 0.0 copy-done.7
  11.9 0.0 copy-start.9
  11.9 1.0 fusion.30
  12.9 0.0 all-gather.6.cloned.1.call-update
  12.9 0.0 all-gather.4.cloned.1.call-start
  13.0 10.7 %all_to_all.46 = bf16[32,32,128]{2,1,0:T(8,128)(2,1)S(1)} all-to-all(bf16[32,32,128]{2,1,0:T(8,128)(2,1)S(1)} %get-tuple-element.8), channel_id=1, replica_groups=mesh['row'=4,'col'=4,'crop'=2] {'row'}, dimensions={0} | all-to-all | bytes 524288 | tf_op jit(solution)/shard_map/all_to_all | solution.py:49
  23.7 21.0 %all_to_all.47 = bf16[32,32,128]{2,1,0:T(8,128)(2,1)S(1)} all-to-all(bf16[32,32,128]{2,1,0:T(8,128)(2,1)S(1)} %all_to_all.46), channel_id=1, replica_groups=mesh['row'=4,'col'=4,'crop'=2] {'col'}, dimensions={0} | all-to-all | bytes 524288 | tf_op jit(solution)/shard_map/all_to_all | solution.py:48
  44.7 0.9 copy.98
  45.6 0.0 all-gather.4.cloned.1.call-update
  45.6 0.0 all-gather.8.cloned.1.call-start
  45.7 1.3 fusion.6
  47.0 2.9 %all-gather.6.cloned.1.call-done = bf16[32,128,128]{2,1,0:T(8,128)(2,1)} async-done(((bf16[32,32,128]{2,1,0:T(8,128)(2,1)}), bf16[32,128,128]{2,1,0:T(8,128)(2,1)}) %all-gather.6.cloned.1.call-update) | async-done | bytes 1048592 | tf_op jit(solution)/shard_map/all_gather | solution.py:56
  49.9 2.7 %copy.99 = bf16[32,128,128]{1,0,2:T(8,128)(2,1)} copy(bf16[32,128,128]{2,1,0:T(8,128)(2,1)} %all-gather.6.cloned.1.call-done) | data formatting | bytes 2097152 | tf_op jit(solution)/shard_map/all_gather | solution.py:56
  52.5 24.4 %all-gather.4.cloned.1.call-done = bf16[32,128,128]{1,0,2:T(8,128)(2,1)} async-done(((bf16[8,128,128]{1,0,2:T(8,128)(2,1)}), bf16[32,128,128]{1,0,2:T(8,128)(2,1)}) %all-gather.4.cloned.1.call-update) | async-done | bytes 1048592 | tf_op jit(solution)/shard_map/all_gather | solution.py:60
  76.9 2.2 %bitcast_reduce_fusion = (f32[32,32]{0,1:T(8,128)S(1)}, f32[128,32,32]{2,1,0:T(8,128)S(1)}) fusion(bf16[32,128,128]{1,0,2:T(8,128)(2,1)} %all-gather.4.cloned.1.call-done, bf16[32,128,128]{1,0,2:T(8,128)(2,1)} %copy.99), kind=kOutput, calls=%fused_computation.3 | convolution fusion | flops 33684480 | bytes 2625536 | tf_op jit(solution)/shard_map/ikh,jkh->ijh/dot_general | solution.py:57
  79.2 0.1 copy.100
  79.2 0.1 copy.101
  79.3 0.3 multiply_reduce_fusion
  79.6 0.1 copy.102
  79.7 0.1 copy.103
  79.8 1.3 multiply_convert_fusion
  81.1 2.7 %copy.104 = bf16[32,32,128]{2,1,0:T(8,128)(2,1)S(1)} copy(bf16[32,32,128]{0,1,2:T(8,128)(2,1)} %multiply_convert_fusion) | data formatting | bytes 524288 | tf_op jit(solution)/shard_map/convert_element_type | solution.py:26
  83.7 0.0 copy-start.4
  83.8 1.4 fusion.63
  85.2 0.4 multiply_reduce_fusion.3
  85.6 0.3 multiply_convert_fusion.3
  85.9 0.0 copy-done.3
  86.0 0.3 fusion.51
  86.3 0.3 fusion.53
  86.5 1.0 fusion.20
  87.6 0.0 all-gather.8.cloned.1.call-update
  87.6 0.1 copy.105
  87.7 13.1 %all_to_all.48 = bf16[32,32,128]{2,0,1:T(8,128)(2,1)S(1)} all-to-all(bf16[32,32,128]{2,0,1:T(8,128)(2,1)S(1)} %copy.105), channel_id=1, replica_groups=mesh['row'=4,'col'=4,'crop'=2] {'col'}, dimensions={1} | all-to-all | bytes 524288 | tf_op jit(solution)/shard_map/all_to_all | solution.py:67
  100.8 8.4 %all_to_all.49 = bf16[32,32,128]{2,0,1:T(8,128)(2,1)S(1)} all-to-all(bf16[32,32,128]{2,0,1:T(8,128)(2,1)S(1)} %all_to_all.48), channel_id=1, replica_groups=mesh['row'=4,'col'=4,'crop'=2] {'row'}, dimensions={1} | all-to-all | bytes 524288 | tf_op jit(solution)/shard_map/all_to_all | solution.py:66
  109.1 0.1 copy.107
  109.2 0.2 copy.108
  109.5 0.2 collective-permute-start
  109.7 0.3 fusion.3
  110.0 3.8 %collective-permute-start.2 = (bf16[128,8,128]{0,1,2:T(8,128)(2,1)S(1)}, bf16[128,8,128]{0,1,2:T(8,128)(2,1)S(1)}, u32[]{:S(2)}, u32[]{:S(2)}) collective-permute-start(bf16[128,8,128]{0,1,2:T(8,128)(2,1)S(1)} %copy.108), channel_id=1, source_target_pairs={{0,6},{2,0},{4,2},{6,4},{1,7},{3,1},{5,3},{7,5},{8,14},{10,8},{12,... | collective-permute-start | bytes 786440 | tf_op jit(solution)/shard_map/ppermute | solution.py:88
  113.7 4.8 %collective-permute-done = bf16[128,8,128]{0,1,2:T(8,128)(2,1)S(1)} collective-permute-done((bf16[128,8,128]{0,1,2:T(8,128)(2,1)S(1)}, bf16[128,8,128]{0,1,2:T(8,128)(2,1)S(1)}, u32[]{:S(2)}, u32[]{:S(2)}) %collective-permute-start) | collective-permute-done | bytes 262176 | tf_op jit(solution)/shard_map/ppermute | solution.py:87
  118.5 0.3 collective-permute-start.1
  118.8 7.3 %copy.109 = bf16[128,32,128]{1,0,2:T(8,128)(2,1)} copy(bf16[128,32,128]{2,1,0:T(8,128)(2,1)} %all-gather.8.cloned.1.call-done) | data formatting | bytes 2097152 | tf_op jit(solution)/shard_map/all_gather | solution.py:74
  126.1 3.5 %convolution_bitcast_fusion.1 = f32[8,32,128]{1,0,2:T(8,128)S(1)} fusion(bf16[128,32,128]{1,0,2:T(8,128)(2,1)} %copy.109, bf16[128,8,128]{0,1,2:T(8,128)(2,1)S(1)} %copy.108), kind=kOutput, calls=%fused_computation.9 | convolution fusion | flops 8388608 | bytes 1441792 | tf_op jit(solution)/shard_map/kih,kjh->ijh/dot_general | solution.py:97
  129.6 0.0 collective-permute-done.2
  129.6 1.2 convolution_bitcast_fusion
  130.8 0.2 copy.118
  131.0 0.2 copy.117
  131.2 3.4 %convolution_bitcast_fusion.2 = f32[8,32,128]{1,0,2:T(8,128)S(1)} fusion(bf16[128,32,128]{1,0,2:T(8,128)(2,1)} %copy.109, bf16[128,8,128]{0,1,2:T(8,128)(2,1)S(1)} %collective-permute-done), kind=kOutput, calls=%fused_computation.10 | convolution fusion | flops 8388608 | bytes 1441792 | tf_op jit(solution)/shard_map/kih,kjh->ijh/dot_general | solution.py:97
  134.6 0.2 copy.116
  134.8 0.0 collective-permute-done.1
  134.8 3.4 %convolution_bitcast_fusion.3 = f32[8,32,128]{1,0,2:T(8,128)S(1)} fusion(bf16[128,32,128]{1,0,2:T(8,128)(2,1)} %copy.109, bf16[128,8,128]{0,1,2:T(8,128)(2,1)S(1)} %collective-permute-done.1), kind=kOutput, calls=%fused_computation.11 | convolution fusion | flops 8388608 | bytes 1441792 | tf_op jit(solution)/shard_map/kih,kjh->ijh/dot_general | solution.py:97
  138.2 0.2 copy.115
  138.6 0.2 dynamic-slice_reduce_fusion
  138.8 0.4 multiply_reduce_fusion.2
  139.2 0.8 fusion.64
  140.1 0.4 multiply_reduce_fusion.1
  140.5 0.0 copy-start.8
  140.5 0.8 fusion.39
  141.3 0.1 copy-done.8
  141.4 1.4 fusion.13
  (38 shorter events, 0.2 us)
Async XLA Ops:
  6.5 134.0 %copy-start = (bf16[128,1024]{1,0:T(8,128)(2,1)S(1)}, bf16[128,1024]{1,0:T(8,128)(2,1)}, u32[]{:S(2)}) copy-start(bf16[128,1024]{1,0:T(8,128)(2,1)} %param.22) | copy-start | bytes 786436
  6.5 4.0 %copy-start.2 = (bf16[32,32,128]{2,1,0:T(8,128)(2,1)S(1)}, bf16[32,32,128]{2,1,0:T(8,128)(2,1)}, u32[]{:S(2)}) copy-start(bf16[32,32,128]{2,1,0:T(8,128)(2,1)} %param.12) | copy-start | bytes 786436
  6.5 5.3 %copy-start.7 = (s32[32,32]{1,0:T(8,128)S(1)}, s32[32,32]{1,0:T(8,128)}, u32[]{:S(2)}) copy-start(s32[32,32]{1,0:T(8,128)} %param.13) | copy-start | bytes 12292
  6.5 43.3 %all-gather.6.cloned.1.call-start = ((), (), s32[]{:S(2)}) async-start(), calls=%async_computation.5 | async-start | bytes 1310720 | tf_op jit(solution)/shard_map/all_gather | solution.py:56
  11.9 33.8 %copy-start.9 = (bf16[128,128]{1,0:T(8,128)(2,1)S(1)}, bf16[128,128]{1,0:T(8,128)(2,1)}, u32[]{:S(2)}) copy-start(bf16[128,128]{1,0:T(8,128)(2,1)} %param.16) | copy-start | bytes 98308
  12.9 64.0 %all-gather.4.cloned.1.call-start = ((), (), s32[]{:S(2)}) async-start(), calls=%async_computation.4 | async-start | bytes 1310720 | tf_op jit(solution)/shard_map/all_gather | solution.py:60
  45.6 73.2 %all-gather.8.cloned.1.call-start = ((), (), s32[]{:S(2)}) async-start(), calls=%async_computation.6 | async-start | bytes 1310720 | tf_op jit(solution)/shard_map/all_gather | solution.py:74
  79.8 3.9 %copy-start.6 = (bf16[128,128]{1,0:T(8,128)(2,1)S(1)}, bf16[128,128]{1,0:T(8,128)(2,1)}, u32[]{:S(2)}) copy-start(bf16[128,128]{1,0:T(8,128)(2,1)} %param.17) | copy-start | bytes 98308
  81.1 4.9 %copy-start.3 = (bf16[128,256]{1,0:T(8,128)(2,1)S(1)}, bf16[128,256]{1,0:T(8,128)(2,1)}, u32[]{:S(2)}) copy-start(bf16[128,256]{1,0:T(8,128)(2,1)} %param.18) | copy-start | bytes 196612
  83.7 2.5 %copy-start.4 = (bf16[128,256]{1,0:T(8,128)(2,1)S(1)}, bf16[128,256]{1,0:T(8,128)(2,1)}, u32[]{:S(2)}) copy-start(bf16[128,256]{1,0:T(8,128)(2,1)} %param.19) | copy-start | bytes 196612
  87.6 22.1 %copy-start.10 = (bf16[128,128]{1,0:T(8,128)(2,1)S(1)}, bf16[128,128]{1,0:T(8,128)(2,1)}, u32[]{:S(2)}) copy-start(bf16[128,128]{1,0:T(8,128)(2,1)} %param.20) | copy-start | bytes 98308
  109.5 9.0 %collective-permute-start = (bf16[128,8,128]{0,1,2:T(8,128)(2,1)S(1)}, bf16[128,8,128]{0,1,2:T(8,128)(2,1)S(1)}, u32[]{:S(2)}, u32[]{:S(2)}) collective-permute-start(bf16[128,8,128]{0,1,2:T(8,128)(2,1)S(1)} %copy.108), channel_id=1, source_target_pairs={{0,2},{2,4},{4,6},{6,0},{1,3},{3,5},{5,7},{7,1},{8,10},{10,12},{12... | collective-permute-start | bytes 786440 | tf_op jit(solution)/shard_map/ppermute | solution.py:87
  110.0 19.7 %collective-permute-start.2 = (bf16[128,8,128]{0,1,2:T(8,128)(2,1)S(1)}, bf16[128,8,128]{0,1,2:T(8,128)(2,1)S(1)}, u32[]{:S(2)}, u32[]{:S(2)}) collective-permute-start(bf16[128,8,128]{0,1,2:T(8,128)(2,1)S(1)} %copy.108), channel_id=1, source_target_pairs={{0,6},{2,0},{4,2},{6,4},{1,7},{3,1},{5,3},{7,5},{8,14},{10,8},{12,... | collective-permute-start | bytes 786440 | tf_op jit(solution)/shard_map/ppermute | solution.py:88
  118.5 16.3 %collective-permute-start.1 = (bf16[128,8,128]{0,1,2:T(8,128)(2,1)S(1)}, bf16[128,8,128]{0,1,2:T(8,128)(2,1)S(1)}, u32[]{:S(2)}, u32[]{:S(2)}) collective-permute-start(bf16[128,8,128]{0,1,2:T(8,128)(2,1)S(1)} %collective-permute-done), channel_id=1, source_target_pairs={{0,2},{2,4},{4,6},{6,0},{1,3},{3,5},{5,7},{7,1},{8,10},{10,12},{12... | collective-permute-start | bytes 786440 | tf_op jit(solution)/shard_map/ppermute | solution.py:87
  126.1 3.5 %copy-start.1 = (bf16[128,32,128]{1,0,2:T(8,128)(2,1)S(1)}, bf16[128,32,128]{1,0,2:T(8,128)(2,1)}, u32[]{:S(2)}) copy-start(bf16[128,32,128]{1,0,2:T(8,128)(2,1)} %copy.109) | copy-start | bytes 3145732
  138.2 1.0 copy-start.5
  140.5 0.9 copy-start.8
Sparse Core Ops, SparseCore 0:
  13.1 36.7 all-gather.5
  51.7 25.2 all-gather.3
  87.7 26.8 all-gather.7
